TPU v7x, 32 devices: a whole 2x2x4 slice. The times are simulated.
32 devices in a mesh: task: 4 (over z), mp: 8 (over y, x, core).
Axes of the slice: x: 2, y: 2, z: 4, core: 2. Of those that a mesh axis runs over, the one named last changes fastest.
Arguments:
- deter: float32 [1024, 4096], P('task', 'mp'), may hold values from -3 to 3
- draws: int32 [4, 32, 1024], P(None, None, 'task'), may hold values from 0 to 31
- actions: int32 [4, 1024], P(None, 'task'), may hold values from 0 to 17
- horizons: int32 [64], replicated, may hold values from 5 to 30, as said below
- offsets: int32 [4, 4], replicated, may hold values from 0 to 3, as said below
- embed_stoch: bfloat16 [1024, 1024], replicated, may hold values from -1 to 1
- embed_act: bfloat16 [18, 1024], replicated, may hold values from -6 to 6
- gru_weight: bfloat16 [5120, 3, 4096], P(None, None, 'mp'), may hold values from -0.078125 to 0.078125
- prior_weight: bfloat16 [4096, 1024], replicated, may hold values from -0.09375 to 0.09375
- logit_weight: bfloat16 [1024, 1024], replicated, may hold values from -0.75 to 0.75
- head_weight: bfloat16 [1024, 2], replicated, may hold values from -0.375 to 0.375
Outputs:
- log_prob: float32 [4, 1024], P(None, 'task')
- reward: float32 [4, 1024], P(None, 'task')
- continuation: float32 [4, 1024], P(None, 'task')
- final_deter: float32 [1024, 4096], P('task', 'mp')
Inputs may be any that keep to these rules, and one draw needn't show every extreme that they name: `horizons`: rows of task k are home rows k * (16) up to (k + 1) * 16 - 1. `offsets`: the 4 numbers of one row are distinct.
All inputs are finite; a program needn't handle non-finite values.
Results may differ from a plain program's by a relative error of at most 0.0045.
Values may be sent and summed in bfloat16 or wider, within the bound.
A program may use at most 128 MiB of HBM per device.

v0:
```python
import jax
import jax.numpy as jnp
from jax import lax
from jax.sharding import PartitionSpec as P

HID = 1024
GROUPS = 32
CLASSES = 32
ACTS = 18
TASKS = 64
BLK_DEV = 4
STEPS = 4
WSTART = 16


def layer_scale(column_sum, squares, entries):
    average = column_sum / entries
    return (average, lax.rsqrt(squares / entries - average * average + 1e-05))


def product(rows_in, weight):
    result = jnp.dot(rows_in, weight, preferred_element_type=jnp.float32)
    return result


def on_device(
    deter,
    draws,
    actions,
    horizons,
    offsets,
    embed_stoch,
    embed_act,
    gru_weight,
    prior_weight,
    logit_weight,
    head_weight,
):
    holders = lax.axis_size("task")
    device = lax.axis_index("task")
    shards = lax.axis_size("mp")
    shard_index = lax.axis_index("mp")
    rows_here = deter.shape[0]
    det_share = deter.shape[1]
    det_full = det_share * shards
    block_rows = rows_here // BLK_DEV
    per_task = rows_here * holders // TASKS
    hid_share = HID // shards
    places = jnp.arange(holders, dtype=jnp.int32)
    local_slot = jnp.arange(BLK_DEV, dtype=jnp.int32)
    within = jnp.arange(block_rows, dtype=jnp.int32)
    classes = jnp.arange(CLASSES, dtype=jnp.int32)
    action_ids = jnp.arange(ACTS, dtype=jnp.int32)
    task_ids = jnp.arange(TASKS, dtype=jnp.int32)
    gate_matrix = gru_weight.reshape(gru_weight.shape[0], 3 * det_share)
    carried = deter
    running = jnp.zeros((BLK_DEV,), jnp.int32)
    logp_list, reward_list, cont_list = ([], [], [])
    for moment in range(STEPS):
        offset_now = offsets[moment]
        target = (device + offset_now) % holders
        sending = (places[:, None] == target[None, :]).astype(jnp.float32)
        outgoing = jnp.einsum(
            "pj,jrc->prc",
            sending,
            carried.reshape(BLK_DEV, block_rows, det_share),
            precision=lax.Precision.HIGHEST,
        )
        arrived = lax.all_to_all(
            outgoing.reshape(holders * block_rows, det_share),
            "task",
            split_axis=0,
            concat_axis=0,
            tiled=True,
        )
        anchor = (device - offset_now) % holders
        taking = (anchor[:, None] == places[None, :]).astype(jnp.float32)
        carried = jnp.einsum(
            "jq,qrc->jrc",
            taking,
            arrived.reshape(holders, block_rows, det_share),
            precision=lax.Precision.HIGHEST,
        ).reshape(rows_here, det_share)
        running = (running + offset_now) % holders
        home_block = (device - running) % holders * BLK_DEV + local_slot
        home_rows = (home_block[:, None] * block_rows + within[None, :]).reshape(rows_here)
        row_task = home_rows // per_task
        horizon_rows = jnp.sum(
            jnp.where(row_task[:, None] == task_ids[None, :], horizons[None, :], 0), axis=1
        )
        living = (horizon_rows > WSTART + moment).astype(jnp.float32)
        chosen_hot = (jnp.transpose(draws[moment])[:, :, None] == classes).astype(jnp.float32)
        stoch_hot = chosen_hot.astype(jnp.bfloat16).reshape(rows_here, GROUPS * CLASSES)
        action_hot = (actions[moment][:, None] == action_ids[None, :]).astype(jnp.bfloat16)
        carried_low = carried.astype(jnp.bfloat16)
        stoch_cols = lax.dynamic_slice_in_dim(embed_stoch, shard_index * hid_share, hid_share, 1)
        act_cols = lax.dynamic_slice_in_dim(embed_act, shard_index * hid_share, hid_share, 1)
        embed_pre = jnp.dot(stoch_hot, stoch_cols, preferred_element_type=jnp.float32) + jnp.dot(
            action_hot, act_cols, preferred_element_type=jnp.float32
        )
        embed_sum, embed_square = lax.psum(
            (jnp.sum(embed_pre, axis=1), jnp.sum(embed_pre * embed_pre, axis=1)), "mp"
        )
        embed_avg, embed_inv = layer_scale(embed_sum, embed_square, HID)
        embed_cols = jax.nn.silu((embed_pre - embed_avg[:, None]) * embed_inv[:, None]).astype(
            jnp.bfloat16
        )
        embedded, gathered = (
            lax.all_gather(embed_cols, "mp", axis=1, tiled=True),
            lax.all_gather(carried_low, "mp", axis=1, tiled=True),
        )
        joined = jnp.concatenate([embedded, gathered], axis=1)
        gate_parts = product(joined, gate_matrix)
        part_sum = jnp.sum(gate_parts, axis=1)
        part_square = jnp.sum(gate_parts * gate_parts, axis=1)
        prior_cols = lax.dynamic_slice_in_dim(prior_weight, shard_index * hid_share, hid_share, 1)
        prior_pre = jnp.dot(gathered, prior_cols, preferred_element_type=jnp.float32)
        part_sum, part_square, prior_sum, prior_square = lax.psum(
            (
                part_sum,
                part_square,
                jnp.sum(prior_pre, axis=1),
                jnp.sum(prior_pre * prior_pre, axis=1),
            ),
            "mp",
        )
        prior_avg, prior_inv = layer_scale(prior_sum, prior_square, HID)
        hidden_cols = jax.nn.silu((prior_pre - prior_avg[:, None]) * prior_inv[:, None]).astype(
            jnp.bfloat16
        )
        hidden = lax.all_gather(hidden_cols, "mp", axis=1, tiled=True)
        gate_avg, gate_inv = layer_scale(part_sum, part_square, 3 * det_full)
        normed = ((gate_parts - gate_avg[:, None]) * gate_inv[:, None]).reshape(
            rows_here, 3, det_share
        )
        reset_gate = jax.nn.sigmoid(normed[:, 0])
        candidate = jnp.tanh(reset_gate * normed[:, 1])
        update = jax.nn.sigmoid(normed[:, 2] - 1.0)
        renewed = update * candidate + (1.0 - update) * carried
        raw_logits = product(hidden, logit_weight).reshape(rows_here, GROUPS, CLASSES)
        capped = 5.0 * jnp.tanh(raw_logits / 5.0)
        exponent = jnp.exp(capped)
        chances = 0.99 * exponent / jnp.sum(exponent, axis=-1, keepdims=True) + 0.01 / CLASSES
        log_prob = jnp.sum(jnp.log(jnp.sum(chances * chosen_hot, axis=-1)), axis=-1) * living
        head_out = jnp.dot(hidden, head_weight, preferred_element_type=jnp.float32)
        logp_list.append(log_prob)
        reward_list.append(head_out[:, 0] * living)
        cont_list.append(jax.nn.sigmoid(head_out[:, 1]) * living)
        carried = jnp.where(living[:, None] > 0, renewed, carried)
    return (jnp.stack(logp_list), jnp.stack(reward_list), jnp.stack(cont_list), carried)


def solution(mesh):
    in_specs = (
        P("task", "mp"),
        P(None, None, "task"),
        P(None, "task"),
        P(),
        P(),
        P(),
        P(),
        P(None, None, "mp"),
        P(),
        P(),
        P(),
    )
    out_specs = (P(None, "task"), P(None, "task"), P(None, "task"), P("task", "mp"))
    return jax.shard_map(
        on_device, mesh=mesh, in_specs=in_specs, out_specs=out_specs, check_vma=False
    )
```

profile of v0, /device:TPU:0, one launch (start us, length us, event | category | flops | bytes accessed | tf_op | source)
XLA Modules:
  0.0 457.5 jit_solution(11337123767255658716)
XLA Ops:
  11.6 6.3 %all-to-all-start = ((f32[4,64,512]{2,1,0:T(8,128)}), f32[4,64,512]{2,1,0:T(8,128)S(1)}, u32[]{:S(2)}, u32[]{:S(2)}) async-start(f32[4,64,512]{2,1,0:T(8,128)} %copy.115), calls=%async_computation | async-start | bytes 1048576 | tf_op jit(solution)/shard_map/all_to_all | solution.py:69
  18.7 13.8 %all-to-all-done = f32[4,64,512]{2,1,0:T(8,128)S(1)} async-done(((f32[4,64,512]{2,1,0:T(8,128)}), f32[4,64,512]{2,1,0:T(8,128)S(1)}, u32[]{:S(2)}, u32[]{:S(2)}) %all-to-all-start) | async-done | bytes 524320 | tf_op jit(solution)/shard_map/all_to_all | solution.py:69
  38.8 13.3 %all-reduce.4 = (f32[256]{0:T(256)S(1)}, f32[256]{0:T(256)S(1)}) all-reduce(f32[256]{0:T(256)S(1)} %get-tuple-element.39, f32[256]{0:T(256)S(1)} %get-tuple-element.38), channel_id=1, replica_groups=mesh['task'=4,'mp'=8] {'mp'}, use_global_device_ids=true, to_apply=%region_12.13 | all-reduce | flops 512 | bytes 4096 | tf_op jit(solution)/shard_map/psum | solution.py:101
  52.1 10.9 %all_gather.38 = bf16[256,1024]{0,1:T(8,128)(2,1)} all-gather(bf16[256,128]{0,1:T(8,128)(2,1)S(1)} %multiply_convert_fusion.6), channel_id=1, replica_groups=mesh['task'=4,'mp'=8] {'mp'}, dimensions={1}, use_global_device_ids=true | all-gather | bytes 589824 | tf_op jit(solution)/shard_map/all_gather | solution.py:109
  63.0 2.1 copy.120
  65.1 21.0 %copy.121 = bf16[5120,3,512]{0,2,1:T(8,128)(2,1)} copy(bf16[5120,3,512]{2,0,1:T(8,128)(2,1)} %param.18) | data formatting | bytes 31457280 | tf_op args[7]
  87.6 11.7 %fusion.221 = (f32[256]{0:T(256)S(1)}, f32[256]{0:T(256)S(1)}, f32[256,1536]{1,0:T(8,128)}) fusion(bf16[5120,1536]{0,1:T(8,128)(2,1)} %bitcast.208, bf16[256,4096]{1,0:T(8,128)(2,1)} %all-gather.5.cloned.1.call-done, bf16[256,1024]{1,0:T(8,128)(2,1)} %copy.120), kind=kOutput, calls=%fused_computation.439 | convolution fusion | flops 4032953856 | bytes 19924992 | tf_op jit(solution)/shard_map/dot_general | solution.py:22
  99.3 13.7 %all-reduce.3 = (f32[256]{0:T(256)S(1)}, f32[256]{0:T(256)S(1)}, f32[256]{0:T(256)S(1)}, f32[256]{0:T(256)S(1)}) all-reduce(f32[256]{0:T(256)S(1)} %get-tuple-element.23, f32[256]{0:T(256)S(1)} %get-tuple-element.22, f32[256]{0:T(256)S(1)} %get-tuple-element.37, f32[256]{0:T(256)S(1)} %get-tuple-element.36), channel_id=1, replica_groups=mesh['task'=4,'mp'=8] {'mp'}, use_global_device_ids=true, to_apply=%region_16.17 | all-reduce | flops 1024 | bytes 8192 | tf_op jit(solution)/shard_map/psum | solution.py:118
  113.0 2.8 subtract_multiply_fusion.3
  115.8 3.1 copy.122
  118.8 2.7 broadcast_subtract_fusion.2
  122.8 2.0 copy.123
  124.8 2.2 fusion.104
  127.2 16.4 %all_to_all.24 = f32[4,64,512]{2,1,0:T(8,128)S(1)} all-to-all(f32[4,64,512]{2,1,0:T(8,128)S(1)} %copy.127), channel_id=1, replica_groups=mesh['task'=4,'mp'=8] {'task'}, dimensions={0} | all-to-all | bytes 1048576 | tf_op jit(solution)/shard_map/all_to_all | solution.py:69
  147.8 10.7 %all_gather.41 = bf16[256,1024]{0,1:T(8,128)(2,1)S(1)} all-gather(bf16[256,128]{0,1:T(8,128)(2,1)S(1)} %multiply_convert_fusion.4), channel_id=1, replica_groups=mesh['task'=4,'mp'=8] {'mp'}, dimensions={1}, use_global_device_ids=true | all-gather | bytes 589824 | tf_op jit(solution)/shard_map/all_gather | solution.py:109
  159.5 12.7 %all-gather.7.cloned.1.call-done = bf16[256,4096]{1,0:T(8,128)(2,1)} async-done(((bf16[256,512]{1,0:T(8,128)(2,1)}), bf16[256,4096]{1,0:T(8,128)(2,1)}) %all-gather.7.cloned.1.call-update) | async-done | bytes 2097168 | tf_op jit(solution)/shard_map/all_gather | solution.py:110
  172.2 11.7 %fusion.220 = (f32[256]{0:T(256)S(1)}, f32[256]{0:T(256)S(1)}, f32[256,1536]{1,0:T(8,128)}) fusion(bf16[5120,1536]{0,1:T(8,128)(2,1)} %bitcast.209, bf16[256,4096]{1,0:T(8,128)(2,1)} %all-gather.7.cloned.1.call-done, bf16[256,1024]{1,0:T(8,128)(2,1)} %copy.132), kind=kOutput, calls=%fused_computation.438 | convolution fusion | flops 4032953856 | bytes 19924992 | tf_op jit(solution)/shard_map/dot_general | solution.py:22
  183.9 13.8 %all-reduce.2 = (f32[256]{0:T(256)S(1)}, f32[256]{0:T(256)S(1)}, f32[256]{0:T(256)}, f32[256]{0:T(256)}) all-reduce(f32[256]{0:T(256)S(1)} %get-tuple-element.21, f32[256]{0:T(256)S(1)} %get-tuple-element.20, f32[256]{0:T(256)S(1)} %get-tuple-element.35, f32[256]{0:T(256)S(1)} %get-tuple-element.34), channel_id=1, replica_groups=mesh['task'=4,'mp'=8] {'mp'}, use_global_device_ids=true, to_apply=%region_32.33 | all-reduce | flops 1024 | bytes 8192 | tf_op jit(solution)/shard_map/psum | solution.py:118
  197.7 2.8 subtract_multiply_fusion.2
  200.5 3.0 copy.133
  203.5 2.7 broadcast_subtract_fusion.1
  209.5 2.2 fusion.99
  211.9 17.6 %all_to_all.25 = f32[4,64,512]{2,1,0:T(8,128)S(1)} all-to-all(f32[4,64,512]{2,1,0:T(8,128)S(1)} %copy.138), channel_id=1, replica_groups=mesh['task'=4,'mp'=8] {'task'}, dimensions={0} | all-to-all | bytes 1048576 | tf_op jit(solution)/shard_map/all_to_all | solution.py:69
  234.4 10.3 %all_gather.44 = bf16[256,1024]{0,1:T(8,128)(2,1)S(1)} all-gather(bf16[256,128]{0,1:T(8,128)(2,1)S(1)} %multiply_convert_fusion.2), channel_id=1, replica_groups=mesh['task'=4,'mp'=8] {'mp'}, dimensions={1}, use_global_device_ids=true | all-gather | bytes 589824 | tf_op jit(solution)/shard_map/all_gather | solution.py:109
  245.7 12.5 %all-gather.9.cloned.1.call-done = bf16[256,4096]{1,0:T(8,128)(2,1)} async-done(((bf16[256,512]{1,0:T(8,128)(2,1)}), bf16[256,4096]{1,0:T(8,128)(2,1)}) %all-gather.9.cloned.1.call-update) | async-done | bytes 2097168 | tf_op jit(solution)/shard_map/all_gather | solution.py:110
  258.2 11.7 %fusion.219 = (f32[256]{0:T(256)S(1)}, f32[256]{0:T(256)S(1)}, f32[256,1536]{1,0:T(8,128)}) fusion(bf16[5120,1536]{0,1:T(8,128)(2,1)} %bitcast.210, bf16[256,4096]{1,0:T(8,128)(2,1)} %all-gather.9.cloned.1.call-done, bf16[256,1024]{1,0:T(8,128)(2,1)} %copy.143), kind=kOutput, calls=%fused_computation.437 | convolution fusion | flops 4032953856 | bytes 19924992 | tf_op jit(solution)/shard_map/dot_general | solution.py:22
  269.9 13.9 %all-reduce.1 = (f32[256]{0:T(256)S(1)}, f32[256]{0:T(256)S(1)}, f32[256]{0:T(256)}, f32[256]{0:T(256)}) all-reduce(f32[256]{0:T(256)S(1)} %get-tuple-element.19, f32[256]{0:T(256)S(1)} %get-tuple-element.18, f32[256]{0:T(256)S(1)} %copy-done.22, f32[256]{0:T(256)S(1)} %get-tuple-element.24), channel_id=1, replica_groups=mesh['task'=4,'mp'=8] {'mp'}, use_global_device_ids=true, to_apply=%region_48.49 | all-reduce | flops 1024 | bytes 8192 | tf_op jit(solution)/shard_map/psum | solution.py:118
  283.8 2.8 subtract_multiply_fusion.1
  286.6 3.0 copy.144
  289.6 2.7 broadcast_subtract_fusion
  293.6 2.0 copy.145
  295.6 2.2 fusion.94
  298.0 17.6 %all_to_all.26 = f32[4,64,512]{2,1,0:T(8,128)S(1)} all-to-all(f32[4,64,512]{2,1,0:T(8,128)S(1)} %copy.149), channel_id=1, replica_groups=mesh['task'=4,'mp'=8] {'task'}, dimensions={0} | all-to-all | bytes 1048576 | tf_op jit(solution)/shard_map/all_to_all | solution.py:69
  318.0 2.8 fusion.223
  320.8 2.1 fusion.224
  323.1 10.4 %all_gather.47 = bf16[256,1024]{0,1:T(8,128)(2,1)S(1)} all-gather(bf16[256,128]{0,1:T(8,128)(2,1)S(1)} %multiply_convert_fusion), channel_id=1, replica_groups=mesh['task'=4,'mp'=8] {'mp'}, dimensions={1}, use_global_device_ids=true | all-gather | bytes 589824 | tf_op jit(solution)/shard_map/all_gather | solution.py:109
  334.5 3.0 fusion.225
  338.5 6.5 %all-gather.11.cloned.1.call-done = bf16[256,4096]{1,0:T(8,128)(2,1)} async-done(((bf16[256,512]{1,0:T(8,128)(2,1)}), bf16[256,4096]{1,0:T(8,128)(2,1)}) %all-gather.11.cloned.1.call-update) | async-done | bytes 2097168 | tf_op jit(solution)/shard_map/all_gather | solution.py:110
  345.0 2.7 fusion.226
  347.7 11.7 %fusion.218 = (f32[256]{0:T(256)S(1)}, f32[256]{0:T(256)S(1)}, f32[256,1536]{1,0:T(8,128)}) fusion(bf16[5120,1536]{0,1:T(8,128)(2,1)} %bitcast.211, bf16[256,4096]{1,0:T(8,128)(2,1)} %all-gather.11.cloned.1.call-done, bf16[256,1024]{1,0:T(8,128)(2,1)} %copy.153), kind=kOutput, calls=%fused_computation.436 | convolution fusion | flops 4032953856 | bytes 19924992 | tf_op jit(solution)/shard_map/dot_general | solution.py:22
  359.4 23.8 %all-reduce = (f32[256]{0:T(256)S(1)}, f32[256]{0:T(256)S(1)}, f32[256]{0:T(256)S(1)}, f32[256]{0:T(256)S(1)}, f32[256]{0:T(256)S(1)}, /*index=5*/f32[256]{0:T(2...) all-reduce(f32[256]{0:T(256)S(1)} %get-tuple-element.33, ...), channel_id=1, replica_groups=mesh['task'=4,'mp'=8] {'mp'}, use_global_device_ids=true, to_apply=%region_52.53 | all-reduce | flops 2560 | bytes 20480 | tf_op jit(solution)/shard_map/psum | solution.py:118
  383.3 9.8 %all_gather.43 = bf16[256,1024]{0,1:T(8,128)(2,1)S(1)} all-gather(bf16[256,128]{0,1:T(8,128)(2,1)S(1)} %multiply_convert_fusion.3), channel_id=1, replica_groups=mesh['task'=4,'mp'=8] {'mp'}, dimensions={1}, use_global_device_ids=true | all-gather | bytes 589824 | tf_op jit(solution)/shard_map/all_gather | solution.py:131
  393.3 8.9 %all_gather.46 = bf16[256,1024]{0,1:T(8,128)(2,1)S(1)} all-gather(bf16[256,128]{0,1:T(8,128)(2,1)S(1)} %multiply_convert_fusion.1), channel_id=1, replica_groups=mesh['task'=4,'mp'=8] {'mp'}, dimensions={1}, use_global_device_ids=true | all-gather | bytes 589824 | tf_op jit(solution)/shard_map/all_gather | solution.py:131
  405.3 9.8 %all_gather.40 = bf16[256,1024]{0,1:T(8,128)(2,1)S(1)} all-gather(bf16[256,128]{0,1:T(8,128)(2,1)S(1)} %multiply_convert_fusion.5), channel_id=1, replica_groups=mesh['task'=4,'mp'=8] {'mp'}, dimensions={1}, use_global_device_ids=true | all-gather | bytes 589824 | tf_op jit(solution)/shard_map/all_gather | solution.py:131
  417.3 8.9 %all_gather.37 = bf16[256,1024]{0,1:T(8,128)(2,1)S(1)} all-gather(bf16[256,128]{0,1:T(8,128)(2,1)S(1)} %multiply_convert_fusion.7), channel_id=1, replica_groups=mesh['task'=4,'mp'=8] {'mp'}, dimensions={1}, use_global_device_ids=true | all-gather | bytes 589824 | tf_op jit(solution)/shard_map/all_gather | solution.py:131
  429.6 3.0 copy.154
  432.6 2.5 copy.152
  445.1 2.1 fusion.237
  (184 shorter events, 56.5 us)
Async XLA Ops:
  7.2 395.3 %copy-start = (bf16[1024,1024]{1,0:T(8,128)(2,1)S(1)}, bf16[1024,1024]{1,0:T(8,128)(2,1)}, u32[]{:S(2)}) copy-start(bf16[1024,1024]{1,0:T(8,128)(2,1)} %param.20) | copy-start | bytes 6291460
  7.2 10.8 %copy-start.19 = (s32[4,4]{1,0:T(4,128)S(1)}, s32[4,4]{1,0:T(4,128)}, u32[]{:S(2)}) copy-start(s32[4,4]{1,0:T(4,128)} %param.15) | copy-start | bytes 196
  10.6 24.2 %copy-start.32 = (s32[64]{0:T(128)S(1)}, s32[64]{0:T(128)}, u32[]{:S(2)}) copy-start(s32[64]{0:T(128)} %param.14) | copy-start | bytes 772
  10.6 25.1 %copy-start.17 = (s32[4,32,256]{2,1,0:T(8,128)S(1)}, s32[4,32,256]{2,1,0:T(8,128)}, u32[]{:S(2)}) copy-start(s32[4,32,256]{2,1,0:T(8,128)} %param.12) | copy-start | bytes 393220
  11.6 20.8 %all-to-all-start = ((f32[4,64,512]{2,1,0:T(8,128)}), f32[4,64,512]{2,1,0:T(8,128)S(1)}, u32[]{:S(2)}, u32[]{:S(2)}) async-start(f32[4,64,512]{2,1,0:T(8,128)} %copy.115), calls=%async_computation | async-start | bytes 1048576 | tf_op jit(solution)/shard_map/all_to_all | solution.py:69
  17.9 69.6 %all-gather.5.cloned.1.call-start = ((), (), s32[]{:S(2)}) async-start(), calls=%async_computation.4 | async-start | bytes 2359296 | tf_op jit(solution)/shard_map/all_gather | solution.py:110
  32.4 4.8 %copy-start.21 = (s32[4,256]{1,0:T(4,128)S(1)}, s32[4,256]{1,0:T(4,128)}, u32[]{:S(2)}) copy-start(s32[4,256]{1,0:T(4,128)} %param.13) | copy-start | bytes 12292
  32.4 4.8 %copy-start.20 = (bf16[18,1024]{1,0:T(8,128)(2,1)S(1)}, bf16[18,1024]{1,0:T(8,128)(2,1)}, u32[]{:S(2)}) copy-start(bf16[18,1024]{1,0:T(8,128)(2,1)} %param.17) | copy-start | bytes 110596
  34.1 138.1 %all-gather.7.cloned.1.call-start = ((), (), s32[]{:S(2)}) async-start(), calls=%async_computation.5 | async-start | bytes 2359296 | tf_op jit(solution)/shard_map/all_gather | solution.py:110
  35.8 3.0 copy-start.9
  35.8 3.0 copy-start.11
  35.8 3.0 copy-start.13
  35.8 3.0 copy-start.15
  127.0 19.5 %copy-start.5 = (bf16[256,1024]{0,1:T(8,128)(2,1)S(1)}, bf16[256,1024]{0,1:T(8,128)(2,1)}, u32[]{:S(2)}) copy-start(bf16[256,1024]{0,1:T(8,128)(2,1)} %get-tuple-element.93) | copy-start | bytes 1572868
  145.4 112.8 %all-gather.9.cloned.1.call-start = ((), (), s32[]{:S(2)}) async-start(), calls=%async_computation.6 | async-start | bytes 2359296 | tf_op jit(solution)/shard_map/all_gather | solution.py:110
  211.7 20.0 %copy-start.4 = (bf16[256,1024]{0,1:T(8,128)(2,1)S(1)}, bf16[256,1024]{0,1:T(8,128)(2,1)}, u32[]{:S(2)}) copy-start(bf16[256,1024]{0,1:T(8,128)(2,1)} %get-tuple-element.91) | copy-start | bytes 1572868
  231.3 113.8 %all-gather.11.cloned.1.call-start = ((), (), s32[]{:S(2)}) async-start(), calls=%async_computation.7 | async-start | bytes 2359296 | tf_op jit(solution)/shard_map/all_gather | solution.py:110
  245.7 24.2 %copy-start.22 = (f32[256]{0:T(256)S(1)}, f32[256]{0:T(256)}, u32[]{:S(2)}) copy-start(f32[256]{0:T(256)} %get-tuple-element.25) | copy-start | bytes 3076
  289.6 6.0 %copy-start.23 = (s32[4]{0:T(128)S(1)}, s32[4]{0:T(128)}, u32[]{:S(2)}) copy-start(s32[4]{0:T(128)} %get-tuple-element.114) | copy-start | bytes 52
  295.6 20.0 %copy-start.24 = (s32[4]{0:T(128)S(1)}, s32[4]{0:T(128)}, u32[]{:S(2)}) copy-start(s32[4]{0:T(128)} %get-tuple-element.107) | copy-start | bytes 52
  317.5 3.3 copy-start.6
  320.8 2.2 copy-start.30
  320.8 2.2 copy-start.31
  347.7 54.4 %copy-start.18 = (bf16[1024,2]{0,1:T(2,128)(2,1)S(1)}, bf16[1024,2]{0,1:T(2,128)(2,1)}, u32[]{:S(2)}) copy-start(bf16[1024,2]{0,1:T(2,128)(2,1)} %param.21) | copy-start | bytes 12292
  426.1 2.1 copy-start.8
  429.6 5.6 %copy-start.16 = (s32[256,32]{0,1:T(8,128)S(1)}, s32[256,32]{0,1:T(8,128)}, u32[]{:S(2)}) copy-start(s32[256,32]{0,1:T(8,128)} %copy-done.15) | copy-start | bytes 98308
  437.1 1.3 copy-start.14
  438.4 2.0 copy-start.2
  440.4 1.3 copy-start.12
  441.7 2.0 copy-start.3
  443.7 1.3 copy-start.10
  445.1 2.1 copy-start.1
  445.1 2.1 copy-start.7
  445.1 2.1 copy-start.29
  447.2 1.5 copy-start.26
  447.2 1.5 copy-start.28
  447.2 1.5 copy-start.27
  447.2 1.5 copy-start.25
Sparse Core Ops, SparseCore 0:
  34.2 28.4 all-gather.4
  145.5 26.6 all-gather.6
  231.4 26.7 all-gather.8
  317.6 27.4 all-gather.10
where the time goes:
time: 466 us; the launch traced here: 457 us
  blocking collectives  210 us (45%)
  matrix products  83.4 us (18%)
  local copies, waits for them, and re-layouts  61.5 us (13%)
  waiting for transfers between devices  45.6 us (10%)
  other arithmetic  35.8 us (8%)
  between operations  14.9 us (3%)
  starting transfers between devices  6.47 us (1%)
    psum x4, blocking collectives, on_device(): lax.psum((part_sum, part_square, jnp.sum(prior_pre, axis=1), jnp.sum(prio...  65.2 us
    dot_general x8, matrix products, product(): result = jnp.dot(rows_in, weight, preferred_element_type=jnp.float32)  53.3 us
    all_to_all x3, blocking collectives, on_device(): lax.all_to_all(outgoing.reshape(holders * block_rows, det_share), 'task',...  51.7 us
    all_gather x4, blocking collectives, on_device(): lax.all_gather(embed_cols, 'mp', axis=1, tiled=True)  42.3 us
    all_gather x4, blocking collectives, on_device(): hidden = lax.all_gather(hidden_cols, 'mp', axis=1, tiled=True)  37.4 us
    all_gather x4, waiting for transfers between devices, on_device(): lax.all_gather(carried_low, 'mp', axis=1, tiled=True)  31.8 us
    unnamed x68, local copies, waits for them, and re-layouts  22.1 us
    all_to_all x1, waiting for transfers between devices, on_device(): lax.all_to_all(outgoing.reshape(holders * block_rows, det_share), 'task',...  13.8 us
  transfers between devices with their start and end apart: 5, of which 4 were waited for; matrix products, arithmetic and copies ran while one was open for 10% of the time, Pallas kernels for 0%

commit v1 on v0

v1 whole, which is shorter than its diff:
```python
import jax
import jax.numpy as jnp
from jax import lax
from jax.sharding import PartitionSpec as P

HID = 1024
GROUPS = 32
CLASSES = 32
ACTS = 18
TASKS = 64
BLK_DEV = 4
STEPS = 4
WSTART = 16


def normed_rows(values):
    entries = values.shape[-1]
    average = jnp.sum(values, axis=-1, keepdims=True) / entries
    squares = jnp.sum(values * values, axis=-1, keepdims=True) / entries
    return (values - average) * lax.rsqrt(squares - average * average + 1e-05)


def product(rows_in, weight):
    return jnp.dot(rows_in, weight, preferred_element_type=jnp.float32)


def recurrence(deter, embedded, gate_weight, living, det_full):
    carried = deter
    rows_here, det_share = deter.shape
    lows = []
    for moment in range(STEPS):
        low = carried.astype(jnp.bfloat16)
        gathered = lax.all_gather(low, "mp", axis=1, tiled=True)
        lows.append(gathered)
        joined = jnp.concatenate([embedded[moment], gathered], axis=1)
        parts = [product(joined, gate_weight[part]) for part in range(3)]
        sums = sum(jnp.sum(part, axis=1) for part in parts)
        squares = sum(jnp.sum(part * part, axis=1) for part in parts)
        sums, squares = lax.psum(jnp.stack([sums, squares]), "mp")
        average = sums / (3 * det_full)
        inverse = lax.rsqrt(squares / (3 * det_full) - average * average + 1e-05)
        normed = [(part - average[:, None]) * inverse[:, None] for part in parts]
        reset_gate = jax.nn.sigmoid(normed[0])
        candidate = jnp.tanh(reset_gate * normed[1])
        update = jax.nn.sigmoid(normed[2] - 1.0)
        renewed = update * candidate + (1.0 - update) * carried
        carried = jnp.where(living[moment][:, None] > 0, renewed, carried)
    return carried, lows


def on_device(
    deter,
    draws,
    actions,
    horizons,
    offsets,
    embed_stoch,
    embed_act,
    gru_weight,
    prior_weight,
    logit_weight,
    head_weight,
):
    holders = lax.axis_size("task")
    device = lax.axis_index("task")
    shards = lax.axis_size("mp")
    shard_index = lax.axis_index("mp")
    rows_here, det_share = deter.shape
    block_rows = rows_here // BLK_DEV
    per_task = rows_here * holders // TASKS
    own_rows = rows_here // shards
    places = jnp.arange(holders, dtype=jnp.int32)
    classes = jnp.arange(CLASSES, dtype=jnp.int32)
    running = jnp.cumsum(offsets, axis=0) % holders
    packed = jnp.concatenate([draws, actions[:, None]], axis=1).astype(jnp.bfloat16)
    packed = lax.all_gather(packed, "task")
    packed = packed.reshape(holders, STEPS, GROUPS + 1, BLK_DEV, block_rows)
    at_slot = (device + running) % holders
    picked = places[:, None, None] == at_slot[None]
    packed = jnp.sum(
        jnp.where(picked[:, :, None, :, None], packed.astype(jnp.float32), 0.0), axis=0
    ).astype(jnp.int32)
    packed = packed.reshape(STEPS, GROUPS + 1, rows_here)
    draws_home = jnp.transpose(packed[:, :GROUPS], (0, 2, 1))
    hot = (draws_home[:, :, :, None] == classes).astype(jnp.bfloat16)
    hot = hot.reshape(STEPS * rows_here, GROUPS * CLASSES)
    action_hot = (
        packed[:, GROUPS].reshape(-1)[:, None] == jnp.arange(ACTS, dtype=jnp.int32)
    ).astype(jnp.bfloat16)
    embed_pre = product(hot, embed_stoch) + product(action_hot, embed_act)
    embedded = jax.nn.silu(normed_rows(embed_pre)).astype(jnp.bfloat16)
    embedded = embedded.reshape(STEPS, rows_here, HID)

    home_rows = device * rows_here + jnp.arange(rows_here, dtype=jnp.int32)
    task_ids = jnp.arange(TASKS, dtype=jnp.int32)
    horizon_rows = jnp.sum(
        jnp.where((home_rows // per_task)[:, None] == task_ids, horizons, 0), axis=1
    )
    alive = horizon_rows[None] > WSTART + jnp.arange(STEPS, dtype=jnp.int32)[:, None]
    living = alive.astype(jnp.float32)

    gate_weight = jnp.transpose(gru_weight, (1, 0, 2))
    carried, lows = recurrence(deter, embedded, gate_weight, living, det_share * shards)

    target = (device + running[-1]) % holders
    sending = places[:, None] == target[None, :]
    blocks = carried.reshape(BLK_DEV, block_rows, det_share)
    outgoing = jnp.where(sending[:, :, None, None], blocks[None], 0.0).astype(jnp.bfloat16)
    arrived = lax.all_to_all(
        outgoing.reshape(holders * BLK_DEV * block_rows, det_share),
        "task",
        split_axis=0,
        concat_axis=0,
        tiled=True,
    ).reshape(holders, BLK_DEV, block_rows, det_share)
    taking = places[:, None] == ((device - running[-1]) % holders)[None, :]
    final = jnp.sum(
        jnp.where(taking[:, :, None, None], arrived.astype(jnp.float32), 0.0), axis=0
    ).reshape(rows_here, det_share)

    def own(array, axis):
        return lax.dynamic_slice_in_dim(array, shard_index * own_rows, own_rows, axis)

    state_rows = jnp.concatenate([own(low, 0) for low in lows], axis=0)
    hidden = jax.nn.silu(normed_rows(product(state_rows, prior_weight))).astype(jnp.bfloat16)
    raw = product(hidden, logit_weight).reshape(STEPS * own_rows, GROUPS, CLASSES)
    exponent = jnp.exp(5.0 * jnp.tanh(raw / 5.0))
    own_hot = own(draws_home, 1).reshape(STEPS * own_rows, GROUPS)[:, :, None] == classes
    chosen = jnp.sum(jnp.where(own_hot, exponent, 0.0), axis=-1)
    chances = 0.99 * chosen / jnp.sum(exponent, axis=-1) + 0.01 / CLASSES
    log_prob = jnp.sum(jnp.log(chances), axis=-1)
    head_out = product(hidden, head_weight)
    results = jnp.stack([log_prob, head_out[:, 0], jax.nn.sigmoid(head_out[:, 1])])
    results = results.reshape(3, STEPS, own_rows) * own(living, 1)[None]
    spread = lax.all_gather(results, ("task", "mp"))
    spread = spread.reshape(holders, shards, 3, STEPS, own_rows)
    spread = jnp.transpose(spread, (0, 2, 3, 1, 4)).reshape(
        holders, 3, STEPS, BLK_DEV, block_rows
    )
    source = (device - running) % holders
    from_home = places[:, None, None] == source[None]
    outs = jnp.sum(jnp.where(from_home[:, None, :, :, None], spread, 0.0), axis=0)
    outs = outs.reshape(3, STEPS, rows_here)
    return (outs[0], outs[1], outs[2], final)


def solution(mesh):
    in_specs = (
        P("task", "mp"),
        P(None, None, "task"),
        P(None, "task"),
        P(),
        P(),
        P(),
        P(),
        P(None, None, "mp"),
        P(),
        P(),
        P(),
    )
    out_specs = (P(None, "task"), P(None, "task"), P(None, "task"), P("task", "mp"))
    return jax.shard_map(
        on_device, mesh=mesh, in_specs=in_specs, out_specs=out_specs, check_vma=False
    )
```

time: 466 us -> 312 us (0.67); the launches traced: 457 us -> 311 us
  blocking collectives: 210 us -> 108 us
  local copies, waits for them, and re-layouts: 61.5 us -> 14.2 us
  waiting for transfers between devices: 45.6 us -> 83 us
  other arithmetic: 35.8 us -> 17.7 us
  matrix products: 83.4 us -> 68.2 us
    all_to_all x3 -> x0, blocking collectives: 51.7 us -> none  [on_device(): lax.all_to_all(outgoing.reshape(holders * block_rows, det_share), 'task',...]
    all_gather x4, waiting for transfers between devices: 31.8 us -> 83 us  [recurrence(): gathered = lax.all_gather(low, 'mp', axis=1, tiled=True)]
    psum x5 -> x4, blocking collectives: 78.5 us -> 52.6 us  [recurrence(): sums, squares = lax.psum(jnp.stack([sums, squares]), 'mp')]
    all_gather x8 -> x2, blocking collectives: 79.7 us -> 55.7 us  [the longest x1 40 us: on_device(): spread = lax.all_gather(results, ('task', 'mp'))]
    unnamed x68 -> x24, local copies, waits for them, and re-layouts: 22.1 us -> 1.12 us
    mul x7 -> x0, local copies, waits for them, and re-layouts: 18.2 us -> none  [the longest x4 12.1 us: on_device(): (gate_parts - gate_avg[:, None]) * gate_inv[:, None]]
    dot_general x32 -> x17, matrix products: 83.4 us -> 68.2 us  [product(): return jnp.dot(rows_in, weight, preferred_element_type=jnp.float32)]
    all_to_all x1, waiting for transfers between devices: 13.8 us -> 0.01 us  [on_device(): lax.all_to_all(outgoing.reshape(holders * BLK_DEV * block_rows, det_share...]
where the time goes in v1:
time: 312 us; the launch traced here: 311 us
  blocking collectives  108 us (35%)
  waiting for transfers between devices  83 us (27%)
  matrix products  68.2 us (22%)
  other arithmetic  17.7 us (6%)
  local copies, waits for them, and re-layouts  14.2 us (5%)
  between operations  14.2 us (5%)
  starting transfers between devices  4.94 us (2%)
    all_gather x4, waiting for transfers between devices, recurrence(): gathered = lax.all_gather(low, 'mp', axis=1, tiled=True)  83 us
    dot_general x17, matrix products, product(): return jnp.dot(rows_in, weight, preferred_element_type=jnp.float32)  68.2 us
    psum x4, blocking collectives, recurrence(): sums, squares = lax.psum(jnp.stack([sums, squares]), 'mp')  52.6 us
    all_gather x1, blocking collectives, on_device(): spread = lax.all_gather(results, ('task', 'mp'))  40 us
    all_gather x1, blocking collectives, on_device(): packed = lax.all_gather(packed, 'task')  15.7 us
    convert_element_type x4, other arithmetic, recurrence(): low = carried.astype(jnp.bfloat16)  8.9 us
  transfers between devices with their start and end apart: 5, of which 4 were waited for; matrix products, arithmetic and copies ran while one was open for 10% of the time, Pallas kernels for 0%

profile of v1, /device:TPU:0, one launch (start us, length us, event | category | flops | bytes accessed | tf_op | source)
XLA Modules:
  0.0 310.5 jit_solution(17363063580489032251)
XLA Ops:
  7.2 1.9 convert_element_type.50
  9.2 0.7 convert_bitcast_fusion
  9.9 0.7 reduce_window_sum.11
  11.0 0.9 convert.10
  12.0 15.7 %all_gather.20 = bf16[4,4,33,256]{3,1,2,0:T(4,128)(2,1)S(1)} all-gather(bf16[1,4,33,256]{3,1,2,0:T(4,128)(2,1)S(1)} %pad_maximum_fusion.16), channel_id=1, replica_groups=mesh['task'=4,'mp'=8] {'task'}, dimensions={0}, use_global_device_ids=true | all-gather | bytes 337920 | tf_op jit(solution)/shard_map/all_gather | solution.py:76
  28.6 1.0 copy.69
  29.6 2.6 fusion
  32.2 1.5 fusion.47
  33.7 1.4 multiply_convert_fusion
  35.1 0.9 fusion.64
  36.5 4.2 %all-gather.5.cloned.1.call-done = bf16[256,4096]{1,0:T(8,128)(2,1)} async-done(((bf16[256,512]{1,0:T(8,128)(2,1)}), bf16[256,4096]{1,0:T(8,128)(2,1)}) %all-gather.5.cloned.1.call-update) | async-done | bytes 2097168 | tf_op jit(solution)/shard_map/all_gather | solution.py:33
  40.7 4.9 %fusion.59 = (f32[256]{0:T(256)S(1)}, f32[256]{0:T(256)S(1)}, f32[256,512]{1,0:T(8,128)S(1)}) fusion(bf16[3,5120,512]{2,1,0:T(8,128)(2,1)} %bitcast.126, bf16[256,4096]{1,0:T(8,128)(2,1)} %all-gather.5.cloned.1.call-done, bf16[256,1024]{1,0:T(8,128)(2,1)S(1)} %copy.60), kind=kOutput, calls=%fused_computation.170 | convolution fusion | flops 1347812864 | bytes 8390656 | tf_op jit(solution)/shard_map/dot_general | solution.py:24
  45.6 4.8 %fusion.58 = (f32[256]{0:T(256)S(1)}, f32[256]{0:T(256)S(1)}, f32[256,512]{1,0:T(8,128)}) fusion(bf16[3,5120,512]{2,1,0:T(8,128)(2,1)} %bitcast.127, bf16[256,4096]{1,0:T(8,128)(2,1)S(1)} %copy-done.5, bf16[256,1024]{1,0:T(8,128)(2,1)S(1)} %copy.60), kind=kOutput, calls=%fused_computation.169 | convolution fusion | flops 1347812864 | bytes 8390656 | tf_op jit(solution)/shard_map/dot_general | solution.py:24
  50.4 4.9 %fusion.60 = (f32[256]{0:T(256)S(1)}, f32[256]{0:T(256)S(1)}, f32[256,512]{1,0:T(8,128)}) fusion(bf16[3,5120,512]{2,1,0:T(8,128)(2,1)} %bitcast.128, bf16[256,4096]{1,0:T(8,128)(2,1)S(1)} %copy-done.5, bf16[256,1024]{1,0:T(8,128)(2,1)S(1)} %copy.60), kind=kOutput, calls=%fused_computation.171 | convolution fusion | flops 1347812864 | bytes 8390656 | tf_op jit(solution)/shard_map/dot_general | solution.py:24
  55.4 13.1 %psum.28 = f32[2,256]{1,0:T(2,128)S(1)} all-reduce(f32[2,256]{1,0:T(2,128)S(1)} %pad_maximum_fusion.17), channel_id=1, replica_groups=mesh['task'=4,'mp'=8] {'mp'}, use_global_device_ids=true, to_apply=%region_11.12 | all-reduce | flops 512 | bytes 4096 | tf_op jit(solution)/shard_map/psum | solution.py:39
  68.5 2.4 fusion.63
  71.3 27.8 %all-gather.7.cloned.1.call-done = bf16[256,4096]{1,0:T(8,128)(2,1)} async-done(((bf16[256,512]{1,0:T(8,128)(2,1)}), bf16[256,4096]{1,0:T(8,128)(2,1)}) %all-gather.7.cloned.1.call-update) | async-done | bytes 2097168 | tf_op jit(solution)/shard_map/all_gather | solution.py:33
  99.1 4.9 %fusion.56 = (f32[256]{0:T(256)S(1)}, f32[256]{0:T(256)S(1)}, f32[256,512]{1,0:T(8,128)S(1)}) fusion(bf16[3,5120,512]{2,1,0:T(8,128)(2,1)} %bitcast.129, bf16[256,4096]{1,0:T(8,128)(2,1)} %all-gather.7.cloned.1.call-done, bf16[256,1024]{1,0:T(8,128)(2,1)S(1)} %copy.61), kind=kOutput, calls=%fused_computation.167 | convolution fusion | flops 1347812864 | bytes 8390656 | tf_op jit(solution)/shard_map/dot_general | solution.py:24
  104.0 4.8 %fusion.55 = (f32[256]{0:T(256)S(1)}, f32[256]{0:T(256)S(1)}, f32[256,512]{1,0:T(8,128)}) fusion(bf16[3,5120,512]{2,1,0:T(8,128)(2,1)} %bitcast.130, bf16[256,4096]{1,0:T(8,128)(2,1)S(1)} %copy-done.6, bf16[256,1024]{1,0:T(8,128)(2,1)S(1)} %copy.61), kind=kOutput, calls=%fused_computation.166 | convolution fusion | flops 1347812864 | bytes 8390656 | tf_op jit(solution)/shard_map/dot_general | solution.py:24
  108.8 4.8 %fusion.57 = (f32[256]{0:T(256)S(1)}, f32[256]{0:T(256)S(1)}, f32[256,512]{1,0:T(8,128)}) fusion(bf16[3,5120,512]{2,1,0:T(8,128)(2,1)} %bitcast.131, bf16[256,4096]{1,0:T(8,128)(2,1)S(1)} %copy-done.6, bf16[256,1024]{1,0:T(8,128)(2,1)S(1)} %copy.61), kind=kOutput, calls=%fused_computation.168 | convolution fusion | flops 1347812864 | bytes 8390656 | tf_op jit(solution)/shard_map/dot_general | solution.py:24
  113.7 13.1 %psum.29 = f32[2,256]{1,0:T(2,128)S(1)} all-reduce(f32[2,256]{1,0:T(2,128)S(1)} %pad_maximum_fusion.18), channel_id=1, replica_groups=mesh['task'=4,'mp'=8] {'mp'}, use_global_device_ids=true, to_apply=%region_18.19 | all-reduce | flops 512 | bytes 4096 | tf_op jit(solution)/shard_map/psum | solution.py:39
  126.8 2.4 fusion.62
  129.4 28.0 %all-gather.9.cloned.1.call-done = bf16[256,4096]{1,0:T(8,128)(2,1)} async-done(((bf16[256,512]{1,0:T(8,128)(2,1)}), bf16[256,4096]{1,0:T(8,128)(2,1)}) %all-gather.9.cloned.1.call-update) | async-done | bytes 2097168 | tf_op jit(solution)/shard_map/all_gather | solution.py:33
  157.4 4.9 %fusion.53 = (f32[256]{0:T(256)S(1)}, f32[256]{0:T(256)S(1)}, f32[256,512]{1,0:T(8,128)S(1)}) fusion(bf16[3,5120,512]{2,1,0:T(8,128)(2,1)} %bitcast.132, bf16[256,4096]{1,0:T(8,128)(2,1)} %all-gather.9.cloned.1.call-done, bf16[256,1024]{1,0:T(8,128)(2,1)S(1)} %copy.62), kind=kOutput, calls=%fused_computation.164 | convolution fusion | flops 1347812864 | bytes 8390656 | tf_op jit(solution)/shard_map/dot_general | solution.py:24
  162.4 4.1 %fusion.52 = (f32[256]{0:T(256)S(1)}, f32[256]{0:T(256)S(1)}, f32[256,512]{1,0:T(8,128)S(1)}) fusion(bf16[3,5120,512]{2,1,0:T(8,128)(2,1)} %bitcast.133, bf16[256,4096]{1,0:T(8,128)(2,1)S(1)} %copy-done.7, bf16[256,1024]{1,0:T(8,128)(2,1)S(1)} %copy.62), kind=kOutput, calls=%fused_computation.163 | convolution fusion | flops 1347812864 | bytes 8390656 | tf_op jit(solution)/shard_map/dot_general | solution.py:24
  166.5 4.8 %fusion.54 = (f32[256]{0:T(256)S(1)}, f32[256]{0:T(256)S(1)}, f32[256,512]{1,0:T(8,128)}) fusion(bf16[3,5120,512]{2,1,0:T(8,128)(2,1)} %bitcast.134, bf16[256,4096]{1,0:T(8,128)(2,1)S(1)} %copy-done.7, bf16[256,1024]{1,0:T(8,128)(2,1)S(1)} %copy.62), kind=kOutput, calls=%fused_computation.165 | convolution fusion | flops 1347812864 | bytes 8390656 | tf_op jit(solution)/shard_map/dot_general | solution.py:24
  171.3 13.1 %psum.30 = f32[2,256]{1,0:T(2,128)S(1)} all-reduce(f32[2,256]{1,0:T(2,128)S(1)} %pad_maximum_fusion.19), channel_id=1, replica_groups=mesh['task'=4,'mp'=8] {'mp'}, use_global_device_ids=true, to_apply=%region_25.26 | all-reduce | flops 512 | bytes 4096 | tf_op jit(solution)/shard_map/psum | solution.py:39
  184.4 2.2 fusion.61
  187.7 1.0 constant_dynamic-slice_fusion.4
  188.7 1.7 constant_dynamic-slice_fusion.3
  190.3 1.7 constant_dynamic-slice_fusion.2
  192.0 22.9 %all-gather.11.cloned.1.call-done = bf16[256,4096]{1,0:T(8,128)(2,1)} async-done(((bf16[256,512]{1,0:T(8,128)(2,1)}), bf16[256,4096]{1,0:T(8,128)(2,1)}) %all-gather.11.cloned.1.call-update) | async-done | bytes 2097168 | tf_op jit(solution)/shard_map/all_gather | solution.py:33
  214.9 4.9 %fusion.49 = (f32[256]{0:T(256)S(1)}, f32[256]{0:T(256)S(1)}, f32[256,512]{1,0:T(8,128)S(1)}) fusion(bf16[3,5120,512]{2,1,0:T(8,128)(2,1)} %bitcast.135, bf16[256,4096]{1,0:T(8,128)(2,1)} %all-gather.11.cloned.1.call-done, bf16[256,1024]{1,0:T(8,128)(2,1)S(1)} %copy.67), kind=kOutput, calls=%fused_computation.160 | convolution fusion | flops 1347812864 | bytes 8390656 | tf_op jit(solution)/shard_map/dot_general | solution.py:24
  219.8 4.1 %fusion.48 = (f32[256]{0:T(256)S(1)}, f32[256]{0:T(256)S(1)}, f32[256,512]{1,0:T(8,128)S(1)}) fusion(bf16[3,5120,512]{2,1,0:T(8,128)(2,1)} %bitcast.136, bf16[256,4096]{1,0:T(8,128)(2,1)S(1)} %copy-done.8, bf16[256,1024]{1,0:T(8,128)(2,1)S(1)} %copy.67), kind=kOutput, calls=%fused_computation.159 | convolution fusion | flops 1347812864 | bytes 8390656 | tf_op jit(solution)/shard_map/dot_general | solution.py:24
  224.0 4.1 %fusion.50 = (f32[256]{0:T(256)S(1)}, f32[256]{0:T(256)S(1)}, f32[256,512]{1,0:T(8,128)S(1)}) fusion(bf16[3,5120,512]{2,1,0:T(8,128)(2,1)} %bitcast.137, bf16[256,4096]{1,0:T(8,128)(2,1)S(1)} %copy-done.8, bf16[256,1024]{1,0:T(8,128)(2,1)S(1)} %copy.67), kind=kOutput, calls=%fused_computation.161 | convolution fusion | flops 1347812864 | bytes 8390656 | tf_op jit(solution)/shard_map/dot_general | solution.py:24
  228.1 13.3 %psum.31 = f32[2,256]{1,0:T(2,128)S(1)} all-reduce(f32[2,256]{1,0:T(2,128)S(1)} %pad_maximum_fusion.20), channel_id=1, replica_groups=mesh['task'=4,'mp'=8] {'mp'}, use_global_device_ids=true, to_apply=%region_38.39 | all-reduce | flops 512 | bytes 4096 | tf_op jit(solution)/shard_map/psum | solution.py:39
  241.9 1.2 select_convert_fusion
  243.1 4.6 %all-to-all-start = ((bf16[4,256,512]{2,1,0:T(8,128)(2,1)}), bf16[4,256,512]{2,1,0:T(8,128)(2,1)S(1)}, u32[]{:S(2)}, u32[]{:S(2)}) async-start(bf16[4,256,512]{2,1,0:T(8,128)(2,1)} %select_convert_fusion), calls=%async_computation | async-start | bytes 2097152 | tf_op jit(solution)/shard_map/all_to_all | solution.py:109
  247.7 1.0 constant_dynamic-slice_fusion.1
  248.7 5.1 %fusion.51 = (f32[128]{0:T(128)S(1)}, f32[128]{0:T(128)S(1)}, f32[128,1024]{1,0:T(8,128)S(1)}) fusion(bf16[4096,1024]{1,0:T(8,128)(2,1)} %param.19, bf16[32,4096]{1,0:T(8,128)(2,1)S(1)} %constant_dynamic-slice_fusion.1, bf16[32,4096]{1,0:T(8,128)(2,1)} %constant_dynamic-slice_fusion.2, bf16[32,4096]{1,0:T(8,128)(2,1)} %constant_dynamic-slice_fusion.3, ...), kind=kOutput, calls=%fused_computation.162 | convolution fusion | flops 1078329088 | bytes 9962496 | tf_op jit(solution)/shard_map/dot_general | solution.py:24
  254.5 2.9 fusion.17
  257.3 2.1 copy.63
  259.4 1.3 select_reduce_fusion.2
  260.8 40.0 %all_gather.25 = f32[32,3,4,32]{3,2,1,0:T(4,128)S(1)} all-gather(f32[1,3,4,32]{3,2,1,0:T(4,128)S(1)} %maximum_multiply_fusion), channel_id=1, replica_groups=mesh['task'=4,'mp'=8] {'task','mp'}, dimensions={0}, use_global_device_ids=true | all-gather | bytes 50688 | tf_op jit(solution)/shard_map/all_gather | solution.py:135
  300.9 0.7 squeeze.17
  301.6 0.7 squeeze.16
  302.3 0.7 squeeze.15
  302.9 1.1 select_reduce_fusion
  (104 shorter events, 5.1 us)
Async XLA Ops:
  7.2 22.4 %copy-start = (bf16[1024,1024]{1,0:T(8,128)(2,1)S(1)}, bf16[1024,1024]{1,0:T(8,128)(2,1)}, u32[]{:S(2)}) copy-start(bf16[1024,1024]{1,0:T(8,128)(2,1)} %param.16) | copy-start | bytes 6291460
  7.2 33.5 %all-gather.5.cloned.1.call-start = ((), (), s32[]{:S(2)}) async-start(), calls=%async_computation.1 | async-start | bytes 2359296 | tf_op jit(solution)/shard_map/all_gather | solution.py:33
  9.2 89.9 %all-gather.7.cloned.1.call-start = ((), (), s32[]{:S(2)}) async-start(), calls=%async_computation.2 | async-start | bytes 2359296 | tf_op jit(solution)/shard_map/all_gather | solution.py:33
  29.6 2.6 copy-start.4
  35.1 1.2 copy-start.10
  40.7 4.9 %copy-start.5 = (bf16[256,4096]{1,0:T(8,128)(2,1)S(1)}, bf16[256,4096]{1,0:T(8,128)(2,1)}, u32[]{:S(2)}) copy-start(bf16[256,4096]{1,0:T(8,128)(2,1)} %all-gather.5.cloned.1.call-done) | copy-start | bytes 6291460
  50.4 18.0 %copy-start.2 = (f32[256,512]{1,0:T(8,128)S(1)}, f32[256,512]{1,0:T(8,128)}, u32[]{:S(2)}) copy-start(f32[256,512]{1,0:T(8,128)} %param.11) | copy-start | bytes 1572868
  50.4 20.7 %copy-start.3 = (bf16[256,1024]{0,1:T(8,128)(2,1)S(1)}, bf16[256,1024]{0,1:T(8,128)(2,1)}, u32[]{:S(2)}) copy-start(bf16[256,1024]{0,1:T(8,128)(2,1)} %get-tuple-element.50) | copy-start | bytes 1572868
  70.9 86.6 %all-gather.9.cloned.1.call-start = ((), (), s32[]{:S(2)}) async-start(), calls=%async_computation.3 | async-start | bytes 2359296 | tf_op jit(solution)/shard_map/all_gather | solution.py:33
  99.1 4.9 %copy-start.6 = (bf16[256,4096]{1,0:T(8,128)(2,1)S(1)}, bf16[256,4096]{1,0:T(8,128)(2,1)}, u32[]{:S(2)}) copy-start(bf16[256,4096]{1,0:T(8,128)(2,1)} %all-gather.7.cloned.1.call-done) | copy-start | bytes 6291460
  129.2 85.7 %all-gather.11.cloned.1.call-start = ((), (), s32[]{:S(2)}) async-start(), calls=%async_computation.4 | async-start | bytes 2359296 | tf_op jit(solution)/shard_map/all_gather | solution.py:33
  157.4 4.9 %copy-start.7 = (bf16[256,4096]{1,0:T(8,128)(2,1)S(1)}, bf16[256,4096]{1,0:T(8,128)(2,1)}, u32[]{:S(2)}) copy-start(bf16[256,4096]{1,0:T(8,128)(2,1)} %all-gather.9.cloned.1.call-done) | copy-start | bytes 6291460
  214.9 4.9 %copy-start.8 = (bf16[256,4096]{1,0:T(8,128)(2,1)S(1)}, bf16[256,4096]{1,0:T(8,128)(2,1)}, u32[]{:S(2)}) copy-start(bf16[256,4096]{1,0:T(8,128)(2,1)} %all-gather.11.cloned.1.call-done) | copy-start | bytes 6291460
  243.1 59.8 %all-to-all-start = ((bf16[4,256,512]{2,1,0:T(8,128)(2,1)}), bf16[4,256,512]{2,1,0:T(8,128)(2,1)S(1)}, u32[]{:S(2)}, u32[]{:S(2)}) async-start(bf16[4,256,512]{2,1,0:T(8,128)(2,1)} %select_convert_fusion), calls=%async_computation | async-start | bytes 2097152 | tf_op jit(solution)/shard_map/all_to_all | solution.py:109
  248.7 5.4 %copy-start.9 = (bf16[1024,2]{0,1:T(2,128)(2,1)S(1)}, bf16[1024,2]{0,1:T(2,128)(2,1)}, u32[]{:S(2)}) copy-start(bf16[1024,2]{0,1:T(2,128)(2,1)} %param.21) | copy-start | bytes 12292
  248.7 55.3 %copy-start.1 = (bf16[1024,1024]{1,0:T(8,128)(2,1)S(1)}, bf16[1024,1024]{1,0:T(8,128)(2,1)}, u32[]{:S(2)}) copy-start(bf16[1024,1024]{1,0:T(8,128)(2,1)} %param.16) | copy-start | bytes 6291460
Sparse Core Ops, SparseCore 0:
  9.9 30.8 all-gather.4
  71.0 28.0 all-gather.6
  129.3 28.0 all-gather.8
  186.8 28.0 all-gather.10

commit v2 on v1

--- a/solution.py
+++ b/solution.py
@@ -1,6 +1,10 @@
+import functools
+
 import jax
 import jax.numpy as jnp
 from jax import lax
+from jax.experimental import pallas as pl
+from jax.experimental.pallas import tpu as pltpu
 from jax.sharding import PartitionSpec as P
 
 HID = 1024
@@ -24,28 +28,217 @@
     return jnp.dot(rows_in, weight, preferred_element_type=jnp.float32)
 
 
-def recurrence(deter, embedded, gate_weight, living, det_full):
-    carried = deter
-    rows_here, det_share = deter.shape
-    lows = []
-    for moment in range(STEPS):
-        low = carried.astype(jnp.bfloat16)
-        gathered = lax.all_gather(low, "mp", axis=1, tiled=True)
-        lows.append(gathered)
-        joined = jnp.concatenate([embedded[moment], gathered], axis=1)
-        parts = [product(joined, gate_weight[part]) for part in range(3)]
-        sums = sum(jnp.sum(part, axis=1) for part in parts)
-        squares = sum(jnp.sum(part * part, axis=1) for part in parts)
-        sums, squares = lax.psum(jnp.stack([sums, squares]), "mp")
-        average = sums / (3 * det_full)
-        inverse = lax.rsqrt(squares / (3 * det_full) - average * average + 1e-05)
-        normed = [(part - average[:, None]) * inverse[:, None] for part in parts]
-        reset_gate = jax.nn.sigmoid(normed[0])
-        candidate = jnp.tanh(reset_gate * normed[1])
-        update = jax.nn.sigmoid(normed[2] - 1.0)
-        renewed = update * candidate + (1.0 - update) * carried
-        carried = jnp.where(living[moment][:, None] > 0, renewed, carried)
-    return carried, lows
+def flipped(index, mask):
+    bit = 1
+    while bit <= mask:
+        if mask & bit:
+            index = index + bit * (1 - 2 * ((index // bit) % 2))
+        bit *= 2
+    return index
+
+
+def window_kernel(
+    shards,
+    groups,
+    rows,
+    share,
+    deter_ref,
+    embedded_ref,
+    living_ref,
+    weight_ref,
+    carried_ref,
+    lows_ref,
+    weight,
+    gath,
+    parts,
+    stats,
+    weight_sem,
+    low_sem,
+    send_sem,
+    recv_sem,
+    stat_send,
+    stat_recv,
+):
+    me = lax.axis_index("mp")
+    peers = {mask: flipped(me, mask) for mask in range(1, shards)}
+    fetch = pltpu.make_async_copy(weight_ref, weight, weight_sem)
+    fetch.start()
+    barrier = pltpu.get_barrier_semaphore()
+    for mask in range(1, shards):
+        pl.semaphore_signal(
+            barrier,
+            inc=1,
+            device_id={"mp": peers[mask]},
+            device_id_type=pl.DeviceIdType.MESH,
+        )
+    bits = []
+    bit = shards // 2
+    while bit:
+        bits.append(bit)
+        bit //= 2
+    orders = [bits, [bits[1], bits[0]] + bits[2:]]
+    half = rows // 2
+    masks = sorted(range(1, shards), key=lambda mask: (mask.bit_count(), mask))
+
+    def source(mask):
+        return me if mask == 0 else peers[mask]
+
+    def hop(g, s, mask, via):
+        block = gath.at[g, source(mask), pl.ds(s * half, half)]
+        return pltpu.make_async_remote_copy(
+            src_ref=block,
+            dst_ref=block,
+            send_sem=send_sem.at[g, s, mask ^ via],
+            recv_sem=recv_sem.at[g, s, mask ^ via],
+            device_id={"mp": peers[via]},
+            device_id_type=pl.DeviceIdType.MESH,
+        )
+
+    def forward(g, s, mask):
+        order = orders[s]
+        last = max([order.index(bit) for bit in order if mask & bit], default=-1)
+        for via in order[last + 1 :]:
+            hop(g, s, mask, via).start()
+
+    def arriving(g, s, mask):
+        block = gath.at[g, source(mask), pl.ds(s * half, half)]
+        return pltpu.make_async_remote_copy(
+            src_ref=block,
+            dst_ref=block,
+            send_sem=send_sem.at[g, s, mask],
+            recv_sem=recv_sem.at[g, s, mask],
+            device_id={"mp": peers[mask]},
+            device_id_type=pl.DeviceIdType.MESH,
+        )
+
+    def launch(g):
+        here = pl.ds(g * rows, rows)
+        gath[g, me] = carried_ref[here, :].astype(jnp.bfloat16)
+        for s in range(2):
+            forward(g, s, 0)
+
+    def stat_copy(g, mask):
+        return pltpu.make_async_remote_copy(
+            src_ref=stats.at[g, 0],
+            dst_ref=stats.at[g, mask],
+            send_sem=stat_send.at[g, mask],
+            recv_sem=stat_recv.at[g, mask],
+            device_id={"mp": peers[mask]},
+            device_id_type=pl.DeviceIdType.MESH,
+        )
+
+    def multiply(g, rows_in, start, depth, first):
+        for part in range(3):
+            term = jnp.dot(
+                rows_in, weight[part, pl.ds(start, depth), :], preferred_element_type=jnp.float32
+            )
+            if first:
+                parts[g, part] = term
+            else:
+                parts[g, part] += term
+
+    carried_ref[...] = deter_ref[...]
+    pl.semaphore_wait(barrier, shards - 1)
+    for g in range(groups):
+        launch(g)
+    fetch.wait()
+
+    def step(t, _):
+        for g in range(groups):
+            seen = set()
+
+            def need(s, mask):
+                if (s, mask) not in seen:
+                    seen.add((s, mask))
+                    arriving(g, s, mask).wait_recv()
+                    forward(g, s, mask)
+
+            multiply(g, embedded_ref[t, pl.ds(g * rows, rows), :], 0, HID, True)
+            for s in range(2):
+                need(s, orders[s][0])
+            for mask in [0] + masks:
+                if mask:
+                    for s in range(2):
+                        need(s, mask)
+                start = pl.multiple_of(HID + source(mask) * share, share)
+                multiply(g, gath[g, source(mask)], start, share, False)
+            keep = pltpu.make_async_copy(gath.at[g], lows_ref.at[t, g], low_sem)
+            keep.start()
+            sums = jnp.zeros((rows, 128), jnp.float32)
+            squares = jnp.zeros((rows, 128), jnp.float32)
+            for part in range(3):
+                for column in range(0, share, 128):
+                    piece = parts[g, part, :, pl.ds(column, 128)]
+                    sums = sums + piece
+                    squares = squares + piece * piece
+            stats[g, 0, 0:1, :] = jnp.sum(sums.T, axis=0, keepdims=True)
+            stats[g, 0, 1:2, :] = jnp.sum(squares.T, axis=0, keepdims=True)
+            for s in range(2):
+                for mask in masks:
+                    arriving(g, s, mask).wait_send()
+            keep.wait()
+            for mask in masks:
+                stat_copy(g, mask).start()
+        for g in range(groups):
+            for mask in masks:
+                stat_copy(g, mask).wait()
+            total = jnp.sum(stats[g], axis=0) / (3 * share * shards)
+            average = jnp.broadcast_to(total[0:1], (128, rows)).T
+            square = jnp.broadcast_to(total[1:2], (128, rows)).T
+            inverse = lax.rsqrt(square - average * average + 1e-05)
+            here = pl.ds(g * rows, rows)
+            alive = living_ref[t, here, :]
+            for column in range(0, share, 128):
+                where = pl.ds(column, 128)
+                normed = [(parts[g, part, :, where] - average) * inverse for part in range(3)]
+                reset_gate = jax.nn.sigmoid(normed[0])
+                candidate = jnp.tanh(reset_gate * normed[1])
+                update = jax.nn.sigmoid(normed[2] - 1.0)
+                before = carried_ref[here, where]
+                renewed = update * candidate + (1.0 - update) * before
+                carried_ref[here, where] = jnp.where(alive > 0, renewed, before)
+
+            @pl.when(t < STEPS - 1)
+            def _():
+                launch(g)
+
+        return 0
+
+    lax.fori_loop(0, STEPS, step, 0)
+
+
+def recurrence(deter, embedded, gate_weight, living, shards):
+    rows_here, share = deter.shape
+    groups = 2
+    rows = rows_here // groups
+    alive = jnp.broadcast_to(living[:, :, None], (STEPS, rows_here, 128))
+    vmem = pl.BlockSpec(memory_space=pltpu.VMEM)
+    hbm = pl.BlockSpec(memory_space=pl.ANY)
+    dma = pltpu.SemaphoreType.DMA
+    return pl.pallas_call(
+        functools.partial(window_kernel, shards, groups, rows, share),
+        out_shape=(
+            jax.ShapeDtypeStruct((rows_here, share), jnp.float32),
+            jax.ShapeDtypeStruct((STEPS, groups, shards, rows, share), jnp.bfloat16),
+        ),
+        in_specs=[vmem, vmem, vmem, hbm],
+        out_specs=(vmem, hbm),
+        scratch_shapes=[
+            pltpu.VMEM(gate_weight.shape, jnp.bfloat16),
+            pltpu.VMEM((groups, shards, rows, share), jnp.bfloat16),
+            pltpu.VMEM((groups, 3, rows, share), jnp.float32),
+            pltpu.VMEM((groups, shards, 2, rows), jnp.float32),
+            dma,
+            dma,
+            dma((groups, 2, shards)),
+            dma((groups, 2, shards)),
+            dma((groups, shards)),
+            dma((groups, shards)),
+        ],
+        compiler_params=pltpu.CompilerParams(
+            collective_id=0, has_side_effects=True, vmem_limit_bytes=48 * 1024 * 1024
+        ),
+    )(deter, embedded, alive, gate_weight)
 
 
 def on_device(
@@ -100,7 +293,7 @@
     living = alive.astype(jnp.float32)
 
     gate_weight = jnp.transpose(gru_weight, (1, 0, 2))
-    carried, lows = recurrence(deter, embedded, gate_weight, living, det_share * shards)
+    carried, lows = recurrence(deter, embedded, gate_weight, living, shards)
 
     target = (device + running[-1]) % holders
     sending = places[:, None] == target[None, :]
@@ -121,7 +314,14 @@
     def own(array, axis):
         return lax.dynamic_slice_in_dim(array, shard_index * own_rows, own_rows, axis)
 
-    state_rows = jnp.concatenate([own(low, 0) for low in lows], axis=0)
+    first = shard_index * own_rows
+    group_rows = lows.shape[3]
+    state_rows = lax.dynamic_slice(
+        lows,
+        (0, first // group_rows, 0, first % group_rows, 0),
+        (STEPS, 1, shards, own_rows, det_share),
+    )
+    state_rows = jnp.transpose(state_rows, (0, 1, 3, 2, 4)).reshape(STEPS * own_rows, -1)
     hidden = jax.nn.silu(normed_rows(product(state_rows, prior_weight))).astype(jnp.bfloat16)
     raw = product(hidden, logit_weight).reshape(STEPS * own_rows, GROUPS, CLASSES)
     exponent = jnp.exp(5.0 * jnp.tanh(raw / 5.0))

time: 312 us -> 169 us (0.54)
  waiting for transfers between devices: 83 us -> 0.01 us
  Pallas kernels: 0 us -> 75 us
  matrix products: 68.2 us -> 11.4 us
  blocking collectives: 108 us -> 57.4 us
  between operations: 14.2 us -> 0.95 us
  other arithmetic: 17.7 us -> 8.64 us
  local copies, waits for them, and re-layouts: 14.2 us -> 9.52 us
    all_gather x4 -> x0, waiting for transfers between devices: 83 us -> none  [recurrence(): gathered = lax.all_gather(low, 'mp', axis=1, tiled=True)]
    pallas_call x0 -> x1, Pallas kernels: none -> 75 us  [recurrence(): pl.pallas_call(functools.partial(window_kernel, shards, groups, rows, sha...]
    dot_general x17 -> x5, matrix products: 68.2 us -> 11.4 us  [product(): return jnp.dot(rows_in, weight, preferred_element_type=jnp.float32)]
    psum x4 -> x0, blocking collectives: 52.6 us -> none  [recurrence(): sums, squares = lax.psum(jnp.stack([sums, squares]), 'mp')]
    convert_element_type x4 -> x0, other arithmetic: 8.9 us -> none  [recurrence(): low = carried.astype(jnp.bfloat16)]
    dynamic_slice x7 -> x3, local copies, waits for them, and re-layouts: 5.51 us -> 0.2 us  [own(): lax.dynamic_slice_in_dim(array, shard_index * own_rows, own_rows, axis)]
  transfers between devices with their start and end apart: 5 -> 1, of which waited for: 4 -> 0; matrix products, arithmetic and copies ran while one was open for 10% -> 10% of each run, Pallas kernels for 0% -> 0%
where the time goes in v2:
time: 169 us; the launch traced here: 168 us
  Pallas kernels  75 us (44%)
  blocking collectives  57.4 us (34%)
  matrix products  11.4 us (7%)
  local copies, waits for them, and re-layouts  9.52 us (6%)
  other arithmetic  8.64 us (5%)
  starting transfers between devices  5.16 us (3%)
    pallas_call x1, Pallas kernels, recurrence(): pl.pallas_call(functools.partial(window_kernel, shards, groups, rows, sha...  75 us
    all_gather x1, blocking collectives, on_device(): spread = lax.all_gather(results, ('task', 'mp'))  41.7 us
    all_gather x1, blocking collectives, on_device(): packed = lax.all_gather(packed, 'task')  15.7 us
    dot_general x5, matrix products, product(): return jnp.dot(rows_in, weight, preferred_element_type=jnp.float32)  11.4 us
    all_to_all x1, starting transfers between devices, on_device(): lax.all_to_all(outgoing.reshape(holders * BLK_DEV * block_rows, det_share...  5.16 us
  transfers between devices with their start and end apart: 1, of which 0 were waited for; matrix products, arithmetic and copies ran while one was open for 10% of the time, Pallas kernels for 0%

profile of v2, /device:TPU:0, one launch (start us, length us, event | category | flops | bytes accessed | tf_op | source)
XLA Modules:
  0.0 168.1 jit_solution(11882931351025139490)
XLA Ops:
  0.7 0.9 reduce_window_sum.11
  1.6 0.7 convert_bitcast_fusion
  2.3 0.1 broadcast_in_dim.117
  2.4 0.1 broadcast_in_dim.118
  2.5 0.9 convert.10
  3.4 0.1 copy.58
  3.4 0.1 pad_maximum_fusion
  3.5 15.7 %all_gather.8 = bf16[4,4,33,256]{3,1,2,0:T(4,128)(2,1)S(1)} all-gather(bf16[1,4,33,256]{3,1,2,0:T(4,128)(2,1)S(1)} %pad_maximum_fusion), channel_id=1, replica_groups=mesh['task'=4,'mp'=8] {'task'}, dimensions={0}, use_global_device_ids=true | all-gather | bytes 337920 | tf_op jit(solution)/shard_map/all_gather | solution.py:269
  19.2 0.2 select_reduce_fusion.1
  19.5 0.1 broadcast_in_dim.129
  19.5 0.1 broadcast_in_dim.130
  19.6 0.1 eq.157
  19.7 0.1 copy.46
  19.8 0.5 eq.154
  20.4 1.0 copy.53
  21.4 0.1 select_reduce_fusion.4
  21.5 0.1 compare_convert_fusion
  21.6 2.5 %fusion = f32[1024,1024]{1,0:T(8,128)S(1)} fusion(bf16[1024,1024]{1,0:T(8,128)(2,1)S(1)} %copy-done, s32[1024,1024]{0,1:T(8,128)S(1)} %bitcast.54, s32[1024]{0:T(1024)S(1)} %eq.157), kind=kOutput, calls=%fused_computation.2 | convolution fusion | flops 2148532224 | bytes 10489856 | tf_op jit(solution)/shard_map/dot_general | solution.py:28
  24.1 1.1 fusion.14
  25.2 1.6 multiply_convert_fusion
  26.8 0.2 broadcast_in_dim.123.living_ref
  27.0 75.0 %shard_map.138 = (f32[256,512]{1,0:T(8,128)S(1)}, bf16[4,2,8,128,512]{4,3,2,1,0:T(8,128)(2,1)}) custom-call(f32[256,512]{1,0:T(8,128)S(1)} %copy-done.1, bf16[4,256,1024]{2,1,0:T(8,128)(2,1)S(1)} %bitcast.50, f32[4,256,128]{2,1,0:T(8,128)S(1)} %broadcast_in_dim.123.living_ref, bf16[3,5120,512]{2,1,0:T(8,128)(2,1)} %bitcast.52), custom_call_target="tpu_custom_call" | custom-call | tf_op jit(solution)/shard_map/pallas_call | solution.py:218
  102.0 1.3 select_convert_fusion
  103.3 5.2 %all-to-all-start = ((bf16[4,256,512]{2,1,0:T(8,128)(2,1)}), bf16[4,256,512]{2,1,0:T(8,128)(2,1)S(1)}, u32[]{:S(2)}, u32[]{:S(2)}) async-start(bf16[4,256,512]{2,1,0:T(8,128)(2,1)} %select_convert_fusion), calls=%async_computation | async-start | bytes 2097152 | tf_op jit(solution)/shard_map/all_to_all | solution.py:302
  108.4 0.1 copy.41
  108.5 0.1 broadcast_in_dim.126
  108.6 0.1 broadcast_in_dim.127
  108.7 0.1 dynamic-slice_bitcast_fusion.1
  108.9 0.1 eq.150
  109.0 1.3 dynamic-slice_bitcast_fusion
  110.3 0.6 copy.47
  110.9 0.4 copy.54
  111.3 4.8 %fusion.15 = (f32[128]{0:T(128)S(1)}, f32[128]{0:T(128)S(1)}, f32[128,1024]{1,0:T(8,128)S(1)}) fusion(bf16[128,4096]{1,0:T(8,128)(2,1)S(1)} %bitcast.53, bf16[4096,1024]{1,0:T(8,128)(2,1)} %param.19), kind=kOutput, calls=%fused_computation.72 | convolution fusion | flops 1074134784 | bytes 9962496 | tf_op jit(solution)/shard_map/dot_general | solution.py:28
  116.1 0.3 multiply_convert_fusion.1
  116.4 0.2 fusion.18
  116.6 0.1 stack.12
  116.7 0.1 stack.13
  116.8 2.9 %fusion.5 = f32[128,1024]{1,0:T(8,128)} fusion(bf16[128,1024]{1,0:T(8,128)(2,1)S(1)} %multiply_convert_fusion.1, bf16[1024,1024]{1,0:T(8,128)(2,1)} %param.20), kind=kOutput, calls=%fused_computation.11 | convolution fusion | flops 268697600 | bytes 2883584 | tf_op jit(solution)/shard_map/dot_general | solution.py:28
  119.7 2.0 %copy.48 = f32[128,1024]{0,1:T(8,128)} copy(f32[128,1024]{1,0:T(8,128)} %fusion.5) | data formatting | bytes 1048576 | tf_op jit(solution)/shard_map/exp | solution.py:327
  121.7 1.3 select_reduce_fusion.2
  123.0 0.1 stack.11
  123.1 0.1 constant_dynamic-slice_fusion
  123.1 41.7 %all_gather.9 = f32[32,3,4,32]{3,2,1,0:T(4,128)S(1)} all-gather(f32[1,3,4,32]{3,2,1,0:T(4,128)S(1)} %maximum_multiply_fusion), channel_id=1, replica_groups=mesh['task'=4,'mp'=8] {'task','mp'}, dimensions={0}, use_global_device_ids=true | all-gather | bytes 50688 | tf_op jit(solution)/shard_map/all_gather | solution.py:335
  164.8 0.1 select_reduce_fusion.3
  165.0 0.7 squeeze.14
  165.7 0.7 squeeze.13
  166.3 0.7 squeeze.12
  167.0 1.1 select_reduce_fusion
  (35 shorter events, 0.3 us)
Async XLA Ops:
  0.6 20.9 %copy-start = (bf16[1024,1024]{1,0:T(8,128)(2,1)S(1)}, bf16[1024,1024]{1,0:T(8,128)(2,1)}, u32[]{:S(2)}) copy-start(bf16[1024,1024]{1,0:T(8,128)(2,1)} %param.16) | copy-start | bytes 6291460
  20.4 1.0 copy-start.4
  21.6 2.5 %copy-start.2 = (bf16[18,1024]{1,0:T(8,128)(2,1)S(1)}, bf16[18,1024]{1,0:T(8,128)(2,1)}, u32[]{:S(2)}) copy-start(bf16[18,1024]{1,0:T(8,128)(2,1)} %param.17) | copy-start | bytes 110596
  25.1 1.8 %copy-start.1 = (f32[256,512]{1,0:T(8,128)S(1)}, f32[256,512]{1,0:T(8,128)}, u32[]{:S(2)}) copy-start(f32[256,512]{1,0:T(8,128)} %deter_ref.1) | copy-start | bytes 1572868
  103.3 63.7 %all-to-all-start = ((bf16[4,256,512]{2,1,0:T(8,128)(2,1)}), bf16[4,256,512]{2,1,0:T(8,128)(2,1)S(1)}, u32[]{:S(2)}, u32[]{:S(2)}) async-start(bf16[4,256,512]{2,1,0:T(8,128)(2,1)} %select_convert_fusion), calls=%async_computation | async-start | bytes 2097152 | tf_op jit(solution)/shard_map/all_to_all | solution.py:302
  111.3 5.1 %copy-start.3 = (bf16[1024,2]{0,1:T(2,128)(2,1)S(1)}, bf16[1024,2]{0,1:T(2,128)(2,1)}, u32[]{:S(2)}) copy-start(bf16[1024,2]{0,1:T(2,128)(2,1)} %param.21) | copy-start | bytes 12292

commit v3 on v2

--- a/solution.py
+++ b/solution.py
@@ -241,6 +241,54 @@
     )(deter, embedded, alive, gate_weight)
 
 
+def spread_kernel(axis, count, block_ref, out_ref, send_sem, recv_sem):
+    me = lax.axis_index(axis)
+    barrier = pltpu.get_barrier_semaphore()
+    for ahead in range(1, count):
+        pl.semaphore_signal(
+            barrier,
+            inc=1,
+            device_id={axis: (me + ahead) % count},
+            device_id_type=pl.DeviceIdType.MESH,
+        )
+    pl.semaphore_wait(barrier, count - 1)
+
+    def copy(ahead, slot):
+        return pltpu.make_async_remote_copy(
+            src_ref=block_ref,
+            dst_ref=out_ref.at[slot],
+            send_sem=send_sem.at[ahead],
+            recv_sem=recv_sem.at[ahead],
+            device_id={axis: (me + ahead) % count},
+            device_id_type=pl.DeviceIdType.MESH,
+        )
+
+    for ahead in range(1, count):
+        copy(ahead, me).start()
+    out_ref[me] = block_ref[...]
+    for ahead in range(1, count):
+        copy(ahead, me).wait_send()
+        copy(ahead, (me + count - ahead) % count).wait_recv()
+
+
+def spread(block, axis, collective_id):
+    count = lax.axis_size(axis)
+    vmem = pl.BlockSpec(memory_space=pltpu.VMEM)
+    return pl.pallas_call(
+        functools.partial(spread_kernel, axis, count),
+        out_shape=jax.ShapeDtypeStruct((count,) + block.shape, block.dtype),
+        in_specs=[vmem],
+        out_specs=vmem,
+        scratch_shapes=[
+            pltpu.SemaphoreType.DMA((count,)),
+            pltpu.SemaphoreType.DMA((count,)),
+        ],
+        compiler_params=pltpu.CompilerParams(
+            collective_id=collective_id, has_side_effects=True
+        ),
+    )(block)
+
+
 def on_device(
     deter,
     draws,
@@ -266,7 +314,7 @@
     classes = jnp.arange(CLASSES, dtype=jnp.int32)
     running = jnp.cumsum(offsets, axis=0) % holders
     packed = jnp.concatenate([draws, actions[:, None]], axis=1).astype(jnp.bfloat16)
-    packed = lax.all_gather(packed, "task")
+    packed = spread(packed, "task", 1)
     packed = packed.reshape(holders, STEPS, GROUPS + 1, BLK_DEV, block_rows)
     at_slot = (device + running) % holders
     picked = places[:, None, None] == at_slot[None]
@@ -332,14 +380,15 @@
     head_out = product(hidden, head_weight)
     results = jnp.stack([log_prob, head_out[:, 0], jax.nn.sigmoid(head_out[:, 1])])
     results = results.reshape(3, STEPS, own_rows) * own(living, 1)[None]
-    spread = lax.all_gather(results, ("task", "mp"))
-    spread = spread.reshape(holders, shards, 3, STEPS, own_rows)
-    spread = jnp.transpose(spread, (0, 2, 3, 1, 4)).reshape(
+    results = spread(results.reshape(3 * STEPS, own_rows), "mp", 2)
+    results = spread(results, "task", 3)
+    results = results.reshape(holders, shards, 3, STEPS, own_rows)
+    results = jnp.transpose(results, (0, 2, 3, 1, 4)).reshape(
         holders, 3, STEPS, BLK_DEV, block_rows
     )
     source = (device - running) % holders
     from_home = places[:, None, None] == source[None]
-    outs = jnp.sum(jnp.where(from_home[:, None, :, :, None], spread, 0.0), axis=0)
+    outs = jnp.sum(jnp.where(from_home[:, None, :, :, None], results, 0.0), axis=0)
     outs = outs.reshape(3, STEPS, rows_here)
     return (outs[0], outs[1], outs[2], final)
 

time: 169 us -> 144 us (0.85)
  blocking collectives: 57.4 us -> 0 us
  Pallas kernels: 75 us -> 104 us
    all_gather x2 -> x0, blocking collectives: 57.4 us -> none  [the longest x1 41.7 us: on_device(): spread = lax.all_gather(results, ('task', 'mp'))]
    pallas_call x0 -> x3, Pallas kernels: none -> 28.9 us  [spread(): pl.pallas_call(functools.partial(spread_kernel, axis, count), out_shape=j...]
  transfers between devices with their start and end apart: 1 -> 1, of which waited for: 0 -> 0; matrix products, arithmetic and copies ran while one was open for 10% -> 13% of each run, Pallas kernels for 0% -> 11%
where the time goes in v3:
time: 144 us; the launch traced here: 143 us
  Pallas kernels  104 us (72%)
  matrix products  11.3 us (8%)
  local copies, waits for them, and re-layouts  11.2 us (8%)
  other arithmetic  10.1 us (7%)
  starting transfers between devices  5.44 us (4%)
    pallas_call x1, Pallas kernels, recurrence(): pl.pallas_call(functools.partial(window_kernel, shards, groups, rows, sha...  75 us
    pallas_call x3, Pallas kernels, spread(): pl.pallas_call(functools.partial(spread_kernel, axis, count), out_shape=j...  28.9 us
    dot_general x5, matrix products, product(): return jnp.dot(rows_in, weight, preferred_element_type=jnp.float32)  11.3 us
    all_to_all x1, starting transfers between devices, on_device(): lax.all_to_all(outgoing.reshape(holders * BLK_DEV * block_rows, det_share...  5.44 us
  transfers between devices with their start and end apart: 1, of which 0 were waited for; matrix products, arithmetic and copies ran while one was open for 13% of the time, Pallas kernels for 11%

profile of v3, /device:TPU:0, one launch (start us, length us, event | category | flops | bytes accessed | tf_op | source)
XLA Modules:
  0.0 142.9 jit_solution(2244708031004843212)
XLA Ops:
  0.7 0.9 reduce_window_sum.11
  1.6 0.7 convert_bitcast_fusion
  2.3 0.1 broadcast_in_dim.120
  2.4 0.1 broadcast_in_dim.121
  2.5 0.9 convert.7
  3.4 0.6 pad_maximum_fusion.block_ref
  4.0 13.0 %shard_map.138 = bf16[4,4,33,256]{3,2,1,0:T(8,128)(2,1)} custom-call(bf16[4,33,256]{2,1,0:T(8,128)(2,1)} %pad_maximum_fusion.block_ref), custom_call_target="tpu_custom_call" | custom-call | tf_op jit(solution)/shard_map/pallas_call | solution.py:277
  17.0 1.1 select_reduce_fusion.1
  18.2 0.1 broadcast_in_dim.133
  18.2 0.1 broadcast_in_dim.134
  18.4 0.1 copy.42
  18.5 0.5 eq.154
  19.1 1.0 copy.46
  20.1 0.1 select_reduce_fusion.4
  20.3 2.5 %fusion = f32[1024,1024]{1,0:T(8,128)S(1)} fusion(bf16[1024,1024]{1,0:T(8,128)(2,1)S(1)} %copy-done, s32[1024,1024]{0,1:T(8,128)S(1)} %bitcast.51, s32[1024]{0:T(1024)S(1)} %eq.157), kind=kOutput, calls=%fused_computation.2 | convolution fusion | flops 2148532224 | bytes 10489856 | tf_op jit(solution)/shard_map/dot_general | solution.py:28
  22.7 1.1 fusion.14
  23.8 1.6 %multiply_convert_fusion = bf16[1024,1024]{1,0:T(8,128)(2,1)S(1)} fusion(f32[1024,1024]{1,0:T(8,128)S(1)} %get-tuple-element.29, f32[1024]{0:T(1024)S(1)} %get-tuple-element.24, f32[1024]{0:T(1024)S(1)} %get-tuple-element.23), kind=kLoop, calls=%fused_computation | loop fusion | flops 7340032 | bytes 6299648 | tf_op jit(solution)/shard_map/convert_element_type | solution.py:332
  25.4 0.2 broadcast_in_dim.127.living_ref
  25.7 75.0 %shard_map.139 = (f32[256,512]{1,0:T(8,128)S(1)}, bf16[4,2,8,128,512]{4,3,2,1,0:T(8,128)(2,1)}) custom-call(f32[256,512]{1,0:T(8,128)S(1)} %copy-done.2, bf16[4,256,1024]{2,1,0:T(8,128)(2,1)S(1)} %bitcast.47, f32[4,256,128]{2,1,0:T(8,128)S(1)} %broadcast_in_dim.127.living_ref, bf16[3,5120,512]{2,1,0:T(8,128)(2,1)} %bitcast.49), custom_call_target="tpu_custom_call" | custom-call | tf_op jit(solution)/shard_map/pallas_call | solution.py:218
  100.7 1.3 select_convert_fusion
  101.9 5.4 %all-to-all-start = ((bf16[4,256,512]{2,1,0:T(8,128)(2,1)}), bf16[4,256,512]{2,1,0:T(8,128)(2,1)S(1)}, u32[]{:S(2)}, u32[]{:S(2)}) async-start(bf16[4,256,512]{2,1,0:T(8,128)(2,1)} %select_convert_fusion), calls=%async_computation | async-start | bytes 2097152 | tf_op jit(solution)/shard_map/all_to_all | solution.py:350
  107.4 0.1 copy.38
  107.5 0.1 broadcast_in_dim.130
  107.6 0.1 broadcast_in_dim.131
  107.6 0.1 copy.39
  107.8 0.1 dynamic-slice_bitcast_fusion.1
  107.9 0.1 eq.150
  108.0 1.3 dynamic-slice_bitcast_fusion
  109.4 0.6 copy.43
  110.0 0.4 copy.47
  110.4 4.7 %fusion.15 = (f32[128]{0:T(128)S(1)}, f32[128]{0:T(128)S(1)}, f32[128,1024]{1,0:T(8,128)S(1)}) fusion(bf16[128,4096]{1,0:T(8,128)(2,1)S(1)} %bitcast.50, bf16[4096,1024]{1,0:T(8,128)(2,1)} %param.19), kind=kOutput, calls=%fused_computation.70 | convolution fusion | flops 1074134784 | bytes 9962496 | tf_op jit(solution)/shard_map/dot_general | solution.py:28
  115.1 0.3 multiply_convert_fusion.1
  115.4 0.2 fusion.18
  115.6 0.1 stack.10
  115.7 0.1 div.76
  115.8 2.9 %fusion.5 = f32[128,1024]{1,0:T(8,128)} fusion(bf16[128,1024]{1,0:T(8,128)(2,1)S(1)} %multiply_convert_fusion.1, bf16[1024,1024]{1,0:T(8,128)(2,1)} %param.20), kind=kOutput, calls=%fused_computation.11 | convolution fusion | flops 268697600 | bytes 2883584 | tf_op jit(solution)/shard_map/dot_general | solution.py:28
  118.7 2.0 %copy.44 = f32[128,1024]{0,1:T(8,128)} copy(f32[128,1024]{1,0:T(8,128)} %fusion.5) | data formatting | bytes 1048576 | tf_op jit(solution)/shard_map/exp | solution.py:375
  120.7 1.3 select_reduce_fusion.2
  122.0 0.1 stack.9
  122.2 0.6 mul.93.block_ref
  122.8 6.0 %shard_map.140.block_ref = f32[8,12,32]{2,1,0:T(8,128)} custom-call(f32[12,32]{1,0:T(8,128)} %mul.93.block_ref), custom_call_target="tpu_custom_call" | custom-call | tf_op jit(solution)/shard_map/pallas_call | solution.py:277
  128.8 9.9 %shard_map.141 = f32[4,8,12,32]{3,2,1,0:T(8,128)} custom-call(f32[8,12,32]{2,1,0:T(8,128)} %shard_map.140.block_ref), custom_call_target="tpu_custom_call" | custom-call | tf_op jit(solution)/shard_map/pallas_call | solution.py:277
  138.7 1.0 copy.45
  139.7 0.1 select_reduce_fusion.3
  139.8 0.7 squeeze.14
  140.5 0.7 squeeze.13
  141.2 0.7 squeeze.12
  141.8 1.1 select_reduce_fusion
  (37 shorter events, 0.5 us)
Async XLA Ops:
  0.6 19.6 %copy-start = (bf16[1024,1024]{1,0:T(8,128)(2,1)S(1)}, bf16[1024,1024]{1,0:T(8,128)(2,1)}, u32[]{:S(2)}) copy-start(bf16[1024,1024]{1,0:T(8,128)(2,1)} %param.16) | copy-start | bytes 6291460
  19.1 1.0 copy-start.5
  20.3 2.5 %copy-start.3 = (bf16[18,1024]{1,0:T(8,128)(2,1)S(1)}, bf16[18,1024]{1,0:T(8,128)(2,1)}, u32[]{:S(2)}) copy-start(bf16[18,1024]{1,0:T(8,128)(2,1)} %param.17) | copy-start | bytes 110596
  23.8 1.8 %copy-start.2 = (f32[256,512]{1,0:T(8,128)S(1)}, f32[256,512]{1,0:T(8,128)}, u32[]{:S(2)}) copy-start(f32[256,512]{1,0:T(8,128)} %deter_ref.1) | copy-start | bytes 1572868
  101.9 39.9 %all-to-all-start = ((bf16[4,256,512]{2,1,0:T(8,128)(2,1)}), bf16[4,256,512]{2,1,0:T(8,128)(2,1)S(1)}, u32[]{:S(2)}, u32[]{:S(2)}) async-start(bf16[4,256,512]{2,1,0:T(8,128)(2,1)} %select_convert_fusion), calls=%async_computation | async-start | bytes 2097152 | tf_op jit(solution)/shard_map/all_to_all | solution.py:350
  110.4 5.0 %copy-start.4 = (bf16[1024,2]{0,1:T(2,128)(2,1)S(1)}, bf16[1024,2]{0,1:T(2,128)(2,1)}, u32[]{:S(2)}) copy-start(bf16[1024,2]{0,1:T(2,128)(2,1)} %param.21) | copy-start | bytes 12292
  115.1 27.8 %copy-start.1 = (bf16[1024,1024]{1,0:T(8,128)(2,1)S(1)}, bf16[1024,1024]{1,0:T(8,128)(2,1)}, u32[]{:S(2)}) copy-start(bf16[1024,1024]{1,0:T(8,128)(2,1)} %param.16) | copy-start | bytes 6291460
